TPU v7x, 32 devices: a whole 2x2x4 slice. The times are simulated.
32 devices in a mesh: seq: 8 (over z, x), head: 4 (over y, core).
Axes of the slice: x: 2, y: 2, z: 4, core: 2. Of those that a mesh axis runs over, the one named last changes fastest.
Arguments:
- queries: bfloat16 [4096, 1024], P('seq', 'head'), may hold values from -6 to 6
- key_vectors: bfloat16 [4096, 1024], P('seq', 'head'), may hold values from -6 to 6
- values: bfloat16 [4096, 2048], P('seq', 'head'), may hold values from -6 to 6
- log_gate: bfloat16 [4096, 1024], P('seq', 'head'), may hold values from -1.6 to 0, as said below
- out_gate: bfloat16 [4096, 2048], P('seq', 'head'), may hold values from -6 to 6
- norm_gain: float32 [2048], P('head'), may hold values from 0.5 to 1.5
- out_weight: bfloat16 [2048, 2048], P('head'), may hold values from -0.1875 to 0.1875
Outputs:
- mixed: bfloat16 [4096, 2048], P('seq', 'head')
Inputs may be any that keep to these rules, and one draw needn't show every extreme that they name: `log_gate`: every entry is below zero.
All inputs are finite; a program needn't handle non-finite values.
Results may differ from a plain program's by a relative error of at most 0.017.
Values may be sent and summed in bfloat16 or wider, within the bound.
A program may use at most 128 MiB of HBM per device.

v0:
```python
import jax
import jax.numpy as jnp
from jax import lax
from jax.sharding import PartitionSpec as P

DK = 256
DV = 512
SPAN = 64


def prefix(shard, axis, join, neutral):
    place = lax.axis_index(axis)
    gathered = jax.tree.map(
        lambda a, kind: lax.all_gather(a.astype(kind), axis), shard, (jnp.bfloat16, jnp.bfloat16)
    )
    state = jax.tree.map(lambda a, e: jnp.zeros_like(a) + jnp.asarray(e, a.dtype), shard, neutral)

    def one(step, state):
        return join(
            state,
            jax.tree.map(
                lambda a, own: lax.dynamic_index_in_dim(a, step, 0, False).astype(own.dtype),
                gathered,
                shard,
            ),
        )

    return lax.fori_loop(0, place, one, state)


def join_states(earlier, latter):
    return (earlier[0] + latter[0], jnp.exp(latter[0])[..., None, :] * earlier[1] + latter[1])


def shards(queries, key_vectors, values, log_gate, out_gate, norm_gain, out_weight):
    length = queries.shape[0]
    head_count = queries.shape[1] // DK
    blocks = length // SPAN
    middle_pos = SPAN // 2
    running = jnp.cumsum(log_gate.astype(jnp.float32).reshape(blocks, SPAN, head_count, DK), axis=1)
    middle = running[:, middle_pos : middle_pos + 1]
    ending = running[:, SPAN - 1 : SPAN]
    query_f = queries.reshape(blocks, SPAN, head_count, DK).astype(jnp.float32)
    key_f = key_vectors.reshape(blocks, SPAN, head_count, DK).astype(jnp.float32)
    q_inter = (query_f * jnp.exp(running)).astype(jnp.bfloat16)
    q_intra = (query_f * jnp.exp(running - middle)).astype(jnp.bfloat16)
    k_intra = (key_f * jnp.exp(middle - running)).astype(jnp.bfloat16)
    k_state = (key_f * jnp.exp(ending - running)).astype(jnp.bfloat16)
    value_blocks = values.reshape(blocks, SPAN, head_count, DV)
    block_state = jnp.einsum(
        "bthe,bthd->bhed", value_blocks, k_state, preferred_element_type=jnp.float32
    )
    block_log = ending[:, 0]
    run_log, run_state = lax.associative_scan(join_states, (block_log, block_state), axis=0)
    device_log = run_log[-1]
    device_state = run_state[-1]
    before_log = run_log - block_log
    before_state = jnp.concatenate([jnp.zeros_like(run_state[:1]), run_state[:-1]], axis=0)
    scores = jnp.einsum("bthd,bshd->bhts", q_intra, k_intra, preferred_element_type=jnp.float32)
    causal = lax.iota(jnp.int32, SPAN)[:, None] >= lax.iota(jnp.int32, SPAN)[None, :]
    weights = jnp.where(causal, scores, 0.0).astype(jnp.bfloat16)
    local_part = jnp.einsum(
        "bhts,bshe->bthe", weights, value_blocks, preferred_element_type=jnp.float32
    )
    zero_log = jnp.zeros_like(device_log)
    zero_state = jnp.zeros_like(device_state)
    incoming_log, incoming = prefix(
        (device_log, device_state), "seq", join_states, (zero_log, zero_state)
    )
    carried = jnp.exp(before_log)[..., None, :] * incoming[None] + before_state
    carried_low = carried.astype(jnp.bfloat16)
    carried_part = jnp.einsum(
        "bthd,bhed->bthe", q_inter, carried_low, preferred_element_type=jnp.float32
    )
    attention = local_part + carried_part
    spread = jnp.mean(attention * attention, axis=-1, keepdims=True)
    normed = attention * lax.rsqrt(spread + 1e-05) * norm_gain.reshape(head_count, DV)
    outer_f = out_gate.reshape(blocks, SPAN, head_count, DV).astype(jnp.float32)
    gated_out = (normed * jax.nn.silu(outer_f)).astype(jnp.bfloat16)
    partial_value = jnp.dot(
        gated_out.reshape(length, head_count * DV), out_weight, preferred_element_type=jnp.float32
    )
    return lax.psum_scatter(
        partial_value.astype(jnp.bfloat16), "head", scatter_dimension=1, tiled=True
    )


def solution(mesh):
    in_specs = (
        P("seq", "head"),
        P("seq", "head"),
        P("seq", "head"),
        P("seq", "head"),
        P("seq", "head"),
        P("head"),
        P("head", None),
    )
    out_specs = P("seq", "head")
    return jax.shard_map(shards, mesh=mesh, in_specs=in_specs, out_specs=out_specs, check_vma=False)
```

profile of v0, /device:TPU:26, one launch (start us, length us, event | category | flops | bytes accessed | tf_op | source)
XLA Modules:
  0.0 144.7 jit_solution(14023225070832756348)
XLA Ops:
  6.5 0.0 copy-start
  6.5 0.0 all-gather.2.cloned.1.call-start
  6.5 1.1 convert.17
  7.7 0.4 fusion.32
  8.1 0.0 copy-start.2
  8.3 0.0 copy-done.8
  8.3 0.0 copy-start.3
  8.4 0.0 copy-done.9
  8.4 1.5 %fusion.29 = (bf16[8,64,256]{2,0,1:T(8,128)(2,1)S(1)}, bf16[8,64,256]{2,0,1:T(8,128)(2,1)}, bf16[8,64,256]{2,0,1:T(8,128)(2,1)}, bf16[8,64,256]{2,0,1:T(8,128)(2,1)S(1)}) fusion(f32[8,64,1,256]{3,0,1,2:T(8,128)S(1)} %fusion.32, f32[8,64,256]{2,1,0:T(8,128)S(1)} %convert.13, f32[8,256]{1,0:T(8,128)S(1)} %get-tuple-element.81, ...), kind=kLoop, calls=%fused_computation.48 | loop fusion | flops 1441792 | bytes 2637824 | tf_op jit(solution)/shard_map/convert_element_type | solution.py:48
  10.0 0.0 copy-done.2
  10.0 0.0 copy-done.3
  10.0 0.8 fusion.35
  10.7 0.0 copy-start.1
  10.7 0.3 slice_add_fusion
  11.0 1.7 %copy-done.1 = f32[8,256,512]{2,1,0:T(8,128)} copy-done((f32[8,256,512]{2,1,0:T(8,128)}, f32[8,256,512]{2,1,0:T(8,128)S(1)}, u32[]{:S(2)}) %copy-start.1) | copy-done | bytes 4194328
  12.7 0.2 slice_add_fusion.1
  12.9 0.1 slice_add_fusion.2
  13.0 0.1 pad_add_fusion
  13.1 0.1 fusion.48
  13.2 1.0 pad_maximum_fusion.1
  14.3 3.5 %pad.47 = f32[4,1,512,256]{2,3,0,1:T(8,128)} pad(f32[2,1,512,256]{2,3,0,1:T(8,128)} %pad_maximum_fusion.1, f32[]{:T(128)} %constant.32.clone.1), padding=0_1_1x0_0_0x0_0_0x0_0_0 | pad | bytes 3145732 | tf_op jit(solution)/shard_map/pad | solution.py:54
  17.7 2.4 %pad.48 = f32[4,1,512,256]{2,3,0,1:T(8,128)} pad(f32[2,1,512,256]{2,3,0,1:T(8,128)S(1)} %pad_add_fusion, f32[]{:T(128)} %constant.32.clone.1), padding=1_0_1x0_0_0x0_0_0x0_0_0 | pad | bytes 3145732 | tf_op jit(solution)/shard_map/pad | solution.py:54
  20.1 4.1 %add.138 = f32[4,1,512,256]{2,3,0,1:T(8,128)} add(f32[4,1,512,256]{2,3,0,1:T(8,128)} %pad.47, f32[4,1,512,256]{2,3,0,1:T(8,128)} %pad.48) | non-fusion elementwise | flops 524288 | bytes 6291456 | tf_op jit(solution)/shard_map/add | solution.py:54
  24.1 5.7 %pad.93 = f32[8,1,512,256]{2,3,0,1:T(8,128)} pad(f32[4,1,512,256]{2,3,0,1:T(8,128)} %add.138, f32[]{:T(128)} %constant.32.clone.1), padding=1_0_1x0_0_0x0_0_0x0_0_0 | pad | bytes 6291460
  29.9 2.6 %fusion.5 = f32[3,1,512,256]{2,3,0,1:T(8,128)S(1)} fusion(f32[4,1,512,256]{2,3,0,1:T(8,128)} %pad.48, f32[4,1,512,256]{2,3,0,1:T(8,128)} %pad.47, f32[8,1,512,256]{2,3,0,1:T(8,128)} %bitcast.95, f32[3,256]{1,0:T(4,128)S(1)} %get-tuple-element.84), kind=kLoop, calls=%fused_computation.11 | loop fusion | flops 1179648 | bytes 6294528 | tf_op jit(solution)/shard_map/add | solution.py:32
  32.5 1.1 slice_bitcast_fusion
  33.6 1.5 %pad_maximum_fusion = f32[4,1,512,256]{2,3,0,1:T(8,128)} fusion(f32[3,1,512,256]{2,3,0,1:T(8,128)S(1)} %fusion.5, f32[1,1,512,256]{2,3,0,1:T(8,128)S(1)} %slice_bitcast_fusion), kind=kLoop, calls=%fused_computation.6 | loop fusion | flops 524288 | bytes 4194304 | tf_op jit(solution)/shard_map/concatenate | solution.py:54
  35.1 5.8 %pad.49 = f32[8,1,512,256]{2,3,0,1:T(8,128)} pad(f32[4,1,512,256]{2,3,0,1:T(8,128)} %pad_maximum_fusion, f32[]{:T(128)} %constant.32.clone.1), padding=0_1_1x0_0_0x0_0_0x0_0_0 | pad | bytes 6291460 | tf_op jit(solution)/shard_map/pad | solution.py:54
  40.8 1.3 add_convert_fusion.1
  42.1 0.8 copy.34
  42.9 0.0 all-gather.2.cloned.1.call-update
  43.0 0.0 reduce-scatter.2.cloned.1.call-start
  43.0 0.0 copy-start.4
  43.0 0.0 copy-start.5
  43.0 0.0 copy-start.6
  43.1 5.6 %pad.61 = f32[7,1,512,256]{2,3,0,1:T(8,128)} pad(f32[4,1,512,256]{2,3,0,1:T(8,128)} %pad_maximum_fusion, f32[]{:T(128)} %constant.32.clone.1), padding=0_0_1x0_0_0x0_0_0x0_0_0 | pad | bytes 5767172 | tf_op jit(solution)/shard_map/slice | solution.py:58
  48.6 0.7 slice_bitcast_fusion.4
  49.4 16.3 %all_gather.8 = bf16[8,1,256]{2,1,0:T(2,128)(2,1)S(1)} all-gather(bf16[1,1,256]{2,1,0:T(2,128)(2,1)S(1)} %fusion.45), channel_id=1, replica_groups=mesh['seq'=8,'head'=4] {'seq'}, dimensions={0}, use_global_device_ids=true | all-gather | bytes 4608 | tf_op jit(solution)/shard_map/all_gather | solution.py:14
  65.6 0.7 exponential_bitcast_fusion
  66.3 0.0 copy-done.4
  66.4 0.0 copy-done.5
  66.4 0.0 copy-done.6
  66.4 1.4 convolution_bitcast_fusion
  67.8 5.8 %slice_add_fusion.4 = f32[7,1,512,256]{2,3,0,1:T(8,128)} fusion(f32[7,1,512,256]{2,3,0,1:T(8,128)} %pad.61, f32[8,1,512,256]{2,3,0,1:T(8,128)} %pad.93), kind=kLoop, calls=%fused_computation.90 | loop fusion | flops 917504 | bytes 11010048 | tf_op jit(solution)/shard_map/add | solution.py:54
  73.6 17.2 %all-gather.2.cloned.1.call-done = bf16[8,1,512,256]{3,2,1,0:T(8,128)(2,1)} async-done(((bf16[1,1,512,256]{3,2,1,0:T(8,128)(2,1)}), bf16[8,1,512,256]{3,2,1,0:T(8,128)(2,1)}) %all-gather.2.cloned.1.call-update) | async-done | bytes 2097168 | tf_op jit(solution)/shard_map/all_gather | solution.py:14
  90.8 8.4 %while.12 = (s32[]{:T(128)}, f32[1,512,256]{2,1,0:T(8,128)S(1)}, s32[]{:T(128)}, bf16[8,1,256]{2,1,0:T(2,128)(2,1)S(1)}, bf16[8,1,512,256]{3,2,1,0:T(8,128)(2,1)}, /*index=5*/s32[]{:T(128)}, s32[]{:T(128)}, s32[]{:T(128)}) while((s32[]{:T(128)}, f32[1,512,256]{2,1,0:T(8,128)S(1)}, s32[]{:T(128)}, bf16[8,1,256]{2,1,0:T(2,128)(2,1)S(1)}, ...), condition=%wide.region_2.3_spmd, body=%wide.region_1.2_spmd.sunk | while | flops 393477 | bytes 1313407 | solution.py:28
  90.9 1.2 convert_add_fusion.2
  92.1 1.2 convert_add_fusion.2
  93.2 1.2 convert_add_fusion.2
  94.4 1.2 convert_add_fusion.2
  95.6 1.2 convert_add_fusion.2
  96.8 1.2 convert_add_fusion.2
  98.0 1.2 convert_add_fusion.2
  99.2 0.2 copy.35
  99.4 0.0 copy-start.7
  99.4 0.0 copy-start.10
  99.4 3.2 %multiply_reduce_fusion = (f32[8,64]{1,0:T(8,128)S(1)}, f32[8,1,512,64]{2,3,0,1:T(8,128)S(1)}) fusion(f32[8,512,64]{1,2,0:T(8,128)} %convolution_bitcast_fusion, f32[7,1,512,256]{2,3,0,1:T(8,128)} %slice_add_fusion.4, f32[512,256]{0,1:T(8,128)S(1)} %copy.35, f32[8,256]{1,0:T(8,128)S(1)} %exponential_bitcast_fusion, ...), kind=kOutput, calls=%fused_computation.27 | convolution fusion | flops 138149376 | bytes 6563840 | tf_op jit(solution)/shard_map/bthd,bhed->bthe/dot_general | solution.py:72
  102.6 0.0 copy-done.7
  102.6 0.0 copy-done.10
  102.6 0.4 fusion.17
  103.0 0.0 copy-done
  103.0 2.6 %convolution_convert_fusion = bf16[512,2048]{1,0:T(8,128)(2,1)} fusion(bf16[512,512]{1,0:T(8,128)(2,1)S(1)} %bitcast.101, bf16[512,2048]{1,0:T(8,128)(2,1)S(1)} %copy-done), kind=kOutput, calls=%fused_computation.3 | convolution fusion | flops 1074790400 | bytes 4718592 | tf_op jit(solution)/shard_map/dot_general | solution.py:80
  105.6 0.0 reduce-scatter.2.cloned.1.call-update
  105.7 32.2 %reduce-scatter.2.cloned.1.call-done = bf16[512,512]{1,0:T(8,128)(2,1)} async-done(((bf16[512,2048]{1,0:T(8,128)(2,1)}), bf16[512,512]{1,0:T(8,128)(2,1)}) %reduce-scatter.2.cloned.1.call-update) | async-done | bytes 524304 | tf_op jit(solution)/shard_map/reduce_scatter | solution.py:83
  (34 shorter events, 0.5 us)
Async XLA Ops:
  6.5 96.5 %copy-start = (bf16[512,2048]{1,0:T(8,128)(2,1)S(1)}, bf16[512,2048]{1,0:T(8,128)(2,1)}, u32[]{:S(2)}) copy-start(bf16[512,2048]{1,0:T(8,128)(2,1)} %param.15) | copy-start | bytes 6291460
  6.5 1.8 %copy-start.8 = (bf16[512,256]{1,0:T(8,128)(2,1)S(1)}, bf16[512,256]{1,0:T(8,128)(2,1)}, u32[]{:S(2)}) copy-start(bf16[512,256]{1,0:T(8,128)(2,1)} %param.10) | copy-start | bytes 786436
  6.5 1.8 %copy-start.9 = (bf16[512,256]{1,0:T(8,128)(2,1)S(1)}, bf16[512,256]{1,0:T(8,128)(2,1)}, u32[]{:S(2)}) copy-start(bf16[512,256]{1,0:T(8,128)(2,1)} %param.9) | copy-start | bytes 786436
  6.5 84.2 %all-gather.2.cloned.1.call-start = ((), (), s32[]{:S(2)}) async-start(), calls=%async_computation.1 | async-start | bytes 2359296 | tf_op jit(solution)/shard_map/all_gather | solution.py:14
  8.1 1.9 %copy-start.2 = (f32[8,64,1,256]{3,0,1,2:T(8,128)}, f32[8,64,1,256]{3,0,1,2:T(8,128)S(1)}, u32[]{:S(2)}) copy-start(f32[8,64,1,256]{3,0,1,2:T(8,128)S(1)} %fusion.32) | copy-start | bytes 1572868
  8.3 1.7 %copy-start.3 = (bf16[512,512]{1,0:T(8,128)(2,1)S(1)}, bf16[512,512]{1,0:T(8,128)(2,1)}, u32[]{:S(2)}) copy-start(bf16[512,512]{1,0:T(8,128)(2,1)} %param.11) | copy-start | bytes 1572868
  10.7 2.0 %copy-start.1 = (f32[8,256,512]{2,1,0:T(8,128)}, f32[8,256,512]{2,1,0:T(8,128)S(1)}, u32[]{:S(2)}) copy-start(f32[8,256,512]{2,1,0:T(8,128)S(1)} %fusion.35) | copy-start | bytes 12582916
  43.0 94.9 %reduce-scatter.2.cloned.1.call-start = ((), (), s32[]{:S(2)}) async-start(), calls=%async_computation.2 | async-start | bytes 2621440 | tf_op jit(solution)/shard_map/reduce_scatter | solution.py:83
  43.0 23.3 %copy-start.4 = (bf16[512,512]{1,0:T(8,128)(2,1)S(1)}, bf16[512,512]{1,0:T(8,128)(2,1)}, u32[]{:S(2)}) copy-start(bf16[512,512]{1,0:T(8,128)(2,1)} %param.11) | copy-start | bytes 1572868
  43.0 23.3 %copy-start.5 = (bf16[8,64,256]{2,0,1:T(8,128)(2,1)S(1)}, bf16[8,64,256]{2,0,1:T(8,128)(2,1)}, u32[]{:S(2)}) copy-start(bf16[8,64,256]{2,0,1:T(8,128)(2,1)} %get-tuple-element.77) | copy-start | bytes 786436
  43.0 23.3 %copy-start.6 = (bf16[8,64,256]{2,0,1:T(8,128)(2,1)S(1)}, bf16[8,64,256]{2,0,1:T(8,128)(2,1)}, u32[]{:S(2)}) copy-start(bf16[8,64,256]{2,0,1:T(8,128)(2,1)} %get-tuple-element.78) | copy-start | bytes 786436
  99.4 3.2 %copy-start.7 = (bf16[512,512]{1,0:T(8,128)(2,1)S(1)}, bf16[512,512]{1,0:T(8,128)(2,1)}, u32[]{:S(2)}) copy-start(bf16[512,512]{1,0:T(8,128)(2,1)} %param.13) | copy-start | bytes 1572868
  99.4 3.2 %copy-start.10 = (f32[512]{0:T(512)S(1)}, f32[512]{0:T(512)}, u32[]{:S(2)}) copy-start(f32[512]{0:T(512)} %param.14) | copy-start | bytes 6148
Sparse Core Ops, SparseCore 0:
  43.1 47.6 all-gather.1
  105.8 32.0 reduce-scatter.1
where the time goes:
time: 147 us; the launch traced here: 145 us
  waiting for transfers between devices  49.5 us (34%)
  other arithmetic  29.5 us (20%)
  local copies, waits for them, and re-layouts  27.7 us (19%)
  blocking collectives  16.3 us (11%)
  between operations  13.7 us (9%)
  matrix products  7.94 us (5%)
    reduce_scatter x1, waiting for transfers between devices, shards(): lax.psum_scatter(partial_value.astype(jnp.bfloat16), 'head', scatter_dime...  32.2 us
    all_gather x1, waiting for transfers between devices, prefix(): lax.all_gather(a.astype(kind), axis)  17.2 us
    all_gather x1, blocking collectives, prefix(): lax.all_gather(a.astype(kind), axis)  16.3 us
    pad x7, local copies, waits for them, and re-layouts, shards(): lax.associative_scan(join_states, (block_log, block_state), axis=0)  11.6 us
    add x11, other arithmetic, join_states(): jnp.exp(latter[0])[..., None, :] * earlier[1] + latter[1]  11.2 us
    add x5, other arithmetic, shards(): lax.associative_scan(join_states, (block_log, block_state), axis=0)  9.95 us
    unnamed x23, local copies, waits for them, and re-layouts  7.49 us
    slice x1, local copies, waits for them, and re-layouts, shards(): run_state[:-1]  5.57 us
  transfers between devices with their start and end apart: 2, of which 2 were waited for; matrix products, arithmetic and copies ran while one was open for 10% of the time, Pallas kernels for 0%

commit v1 on v0

v1 whole, which is shorter than its diff:
```python
import functools

import jax
import jax.numpy as jnp
from jax import lax
from jax.experimental import pallas as pl
from jax.experimental.pallas import tpu as pltpu
from jax.sharding import PartitionSpec as P

DK = 256
DV = 512
SPAN = 64
CHUNKS = 4
TOKENS = 128
F32 = jnp.float32
BF16 = jnp.bfloat16
MESH = pl.DeviceIdType.MESH


def dot(a, b, dims=((1,), (0,))):
    return lax.dot_general(a, b, (dims, ((), ())), preferred_element_type=F32)


def kernel(
    n_seq, n_head,
    q_hbm, k_hbm, v_hbm, g_hbm, o_hbm, gain_hbm, w_hbm,
    out_hbm,
    q, k, v, g, o, gain, w,
    run, ends, kd, qg, att, act, state,
    log_out, log_in, half_out, half_in, own_half, chain_out, chain_in, pass_out, carry,
    gated, mine, y_out, y_in, out,
    load_sem, w_sem, w_send, w_recv, log_sem, half_send, half_recv,
    chain_send, chain_recv, pass_send, pass_recv, g_send, g_recv, y_send, y_recv, out_sem,
):
    length = q.shape[0]
    blocks = length // SPAN
    pieces = length // TOKENS
    groups = n_head // 2
    width = w_hbm.shape[1] // n_head
    half = DV // 2
    rows = half // CHUNKS
    seq = lax.axis_index("seq")
    head = lax.axis_index("head")
    x = lax.rem(seq, 2)
    z = lax.div(seq, 2)
    last = n_seq // 2 - 1
    core = lax.rem(head, 2)
    group = lax.div(head, 2)
    across = {"seq": seq + 1 - 2 * x, "head": head}
    onward = {"seq": lax.rem(seq + 2, n_seq), "head": head}
    back = {"seq": lax.rem(seq + n_seq - 2, n_seq), "head": head}
    partner = {"seq": seq, "head": head + 1 - 2 * core}
    peers = [
        {"seq": seq, "head": lax.rem(head + 2 * step, n_head)} for step in range(1, groups)
    ]

    def columns(which_group, which_core):
        return pl.ds(pl.multiple_of((which_group * 2 + which_core) * width, 128), width)

    loads = [
        pltpu.make_async_copy(src, dst, load_sem.at[i])
        for i, (src, dst) in enumerate(
            ((g_hbm, g), (k_hbm, k), (v_hbm, v), (q_hbm, q), (o_hbm, o), (gain_hbm, gain))
        )
    ]
    for load in loads:
        load.start()
    w_loads = [
        pltpu.make_async_copy(
            w_hbm.at[:, columns(lax.rem(group + j, groups), core)], w.at[0, j], w_sem.at[j]
        )
        for j in range(groups)
    ]
    barrier = pltpu.get_barrier_semaphore()
    friends = [across, onward, back, partner] + peers
    for friend in friends:
        pl.semaphore_signal(barrier, inc=1, device_id=friend, device_id_type=MESH)

    def remote(src, dst, send, recv, device):
        return pltpu.make_async_remote_copy(
            src_ref=src, dst_ref=dst, send_sem=send, recv_sem=recv,
            device_id=device, device_id_type=MESH,
        )

    @pl.when(z == 0)
    def _():
        chain_in[...] = jnp.zeros_like(chain_in)

    tri = (
        lax.broadcasted_iota(jnp.int32, (SPAN, SPAN), 0)
        >= lax.broadcasted_iota(jnp.int32, (SPAN, SPAN), 1)
    )
    ones = jnp.where(tri, 1.0, 0.0).astype(BF16)
    loads[0].wait()
    total = jnp.zeros((1, DK), F32)
    endings = []
    for b in range(blocks):
        r = dot(ones, g[b * SPAN : (b + 1) * SPAN, :])
        run[b] = r
        endings.append(r[SPAN - 1 : SPAN, :])
        ends[b : b + 1, :] = total
        total = total + endings[b]
    log_out[...] = jnp.broadcast_to(total, log_out.shape)
    loads[1].wait()
    tail = jnp.zeros((1, DK), F32)
    for b in reversed(range(blocks)):
        part = slice(b * SPAN, (b + 1) * SPAN)
        kd[part, :] = (k[part, :].astype(F32) * jnp.exp((endings[b] - run[b]) + tail)).astype(BF16)
        tail = tail + endings[b]

    pl.semaphore_wait(barrier, len(friends))
    log_copy = remote(log_out, log_in, log_sem.at[0], log_sem.at[1], across)
    log_copy.start()
    loads[2].wait()

    def half_state(which):
        cols = pl.ds(pl.multiple_of(which * half, 128), half)
        return dot(v[:, cols], kd[...], ((0,), (0,)))

    theirs = half_state(1 - x).astype(BF16)
    half_copies = []
    for i in range(CHUNKS):
        half_out[i] = theirs[i * rows : (i + 1) * rows, :]
        copy = remote(half_out.at[i], half_in.at[i], half_send.at[i], half_recv.at[i], across)
        copy.start()
        half_copies.append(copy)
    own_half[...] = half_state(x).reshape(CHUNKS, rows, DK)
    for load in w_loads:
        load.start()
    w_copies = [
        remote(
            w_hbm.at[:, columns(lax.rem(group + j, groups), 1 - core)], w.at[1, j],
            w_send.at[j], w_recv.at[j], partner,
        )
        for j in range(groups)
    ]
    for copy in w_copies:
        copy.start()

    for load in loads[3:]:
        load.wait()
    state[...] = jnp.zeros_like(state)

    def local(b, _):
        part = pl.ds(pl.multiple_of(b * SPAN, SPAN), SPAN)
        r = run[b]
        middle = r[SPAN // 2 : SPAN // 2 + 1, :]
        ending = r[SPAN - 1 : SPAN, :]
        before = ends[pl.ds(b, 1), :]
        qf = q[part, :].astype(F32)
        kf = k[part, :].astype(F32)
        qi = qf * jnp.exp(r)
        qg[part, :] = (qi * jnp.exp(before)).astype(BF16)
        q_intra = (qf * jnp.exp(r - middle)).astype(BF16)
        k_intra = (kf * jnp.exp(middle - r)).astype(BF16)
        k_state = (kf * jnp.exp(ending - r)).astype(BF16)
        vb = v[part, :]
        scores = dot(q_intra, k_intra, ((1,), (1,)))
        weights = jnp.where(tri, scores, 0.0).astype(BF16)
        held = state[...]
        att[part, :] = dot(weights, vb) + dot(qi.astype(BF16), held.astype(BF16), ((1,), (1,)))
        state[...] = held * jnp.exp(ending) + dot(vb, k_state, ((0,), (0,)))
        of = o[part, :].astype(F32)
        act[part, :] = of / (1.0 + jnp.exp(-of)) * gain[...]
        return 0

    lax.fori_loop(0, blocks, local, 0)

    log_copy.wait()
    mine_log = log_out[0:1, :]
    their_log = log_in[0:1, :]
    first = x == 0
    decay0 = jnp.exp(jnp.where(first, mine_log, their_log))
    decay1 = jnp.exp(jnp.where(first, their_log, mine_log))
    chain_copies = []
    pass_copies = []
    for i in range(CHUNKS):
        half_copies[i].wait_recv()
        chain = remote(
            chain_out.at[i], chain_in.at[i], chain_send.at[i], chain_recv.at[i], onward
        )
        chain_copies.append(chain)
        own = own_half[i]
        other = half_in[i].astype(F32)
        s0 = jnp.where(first, own, other)
        s1 = jnp.where(first, other, own)

        @pl.when(z > 0)
        def _():
            chain.wait_recv()

        entering = chain_in[i].astype(F32)
        between = decay0 * entering + s0
        chain_out[i] = (decay1 * between + s1).astype(BF16)

        @pl.when(z < last)
        def _():
            chain.start()

        pass_out[i] = jnp.where(first, between, entering).astype(BF16)
        carry[x, i] = jnp.where(first, entering, between).astype(BF16)
        passing = remote(
            pass_out.at[i], carry.at[x, i], pass_send.at[i], pass_recv.at[i], across
        )
        passing.start()
        pass_copies.append(passing)
    for passing in pass_copies:
        passing.wait_recv()
    carried = carry[...].reshape(DV, DK)

    g_copies = []
    for i in range(pieces):
        part = slice(i * TOKENS, (i + 1) * TOKENS)
        a = att[part, :] + dot(qg[part, :], carried, ((1,), (1,)))
        spread = jnp.mean(a * a, axis=-1, keepdims=True)
        gated[0, part, :] = (a * lax.rsqrt(spread + 1e-05) * act[part, :]).astype(BF16)
        copy = remote(
            gated.at[0, part, :], gated.at[1, part, :], g_send.at[i], g_recv.at[i], partner
        )
        copy.start()
        g_copies.append(copy)
    for copy in w_loads:
        copy.wait()
    for copy in w_copies:
        copy.wait_recv()
    y_copies = []
    for i in range(pieces):
        part = slice(i * TOKENS, (i + 1) * TOKENS)
        g_copies[i].wait_recv()
        for j in range(1, groups):
            y_out[j - 1, part, :] = (
                dot(gated[0, part, :], w[0, j]) + dot(gated[1, part, :], w[1, j])
            ).astype(BF16)
            copy = remote(
                y_out.at[j - 1, part, :], y_in.at[j - 1, part, :],
                y_send.at[j - 1, i], y_recv.at[j - 1, i], peers[j - 1],
            )
            copy.start()
            y_copies.append(copy)
    for i in range(pieces):
        part = slice(i * TOKENS, (i + 1) * TOKENS)
        mine[part, :] = dot(gated[0, part, :], w[0, 0]) + dot(gated[1, part, :], w[1, 0])
    stores = []
    for i in range(pieces):
        part = slice(i * TOKENS, (i + 1) * TOKENS)
        total_out = mine[part, :]
        for j in range(1, groups):
            y_copies[i * (groups - 1) + j - 1].wait_recv()
            total_out = total_out + y_in[j - 1, part, :].astype(F32)
        out[part, :] = total_out.astype(BF16)
        store = pltpu.make_async_copy(out.at[part, :], out_hbm.at[part, :], out_sem.at[i])
        store.start()
        stores.append(store)
    for copy in half_copies + pass_copies + w_copies + g_copies + y_copies:
        copy.wait_send()

    @pl.when(z < last)
    def _():
        for chain in chain_copies:
            chain.wait_send()

    for store in stores:
        store.wait()


def shards(n_seq, n_head, queries, key_vectors, values, log_gate, out_gate, norm_gain, out_weight):
    length = queries.shape[0]
    width = out_weight.shape[1] // n_head
    groups = n_head // 2
    blocks = length // SPAN
    pieces = length // TOKENS
    half_rows = DV // 2 // CHUNKS
    VM = pltpu.VMEM
    dma = pltpu.SemaphoreType.DMA
    piece_state = (CHUNKS, half_rows, DK)
    scratch = [
        VM((length, DK), BF16), VM((length, DK), BF16), VM((length, DV), BF16),
        VM((length, DK), BF16), VM((length, DV), BF16), VM((1, DV), F32),
        VM((2, groups, DV, width), BF16),
        VM((blocks, SPAN, DK), F32), VM((blocks, DK), F32), VM((length, DK), BF16),
        VM((length, DK), BF16), VM((length, DV), F32), VM((length, DV), F32), VM((DV, DK), F32),
        VM((8, DK), F32), VM((8, DK), F32), VM(piece_state, BF16), VM(piece_state, BF16),
        VM(piece_state, F32), VM(piece_state, BF16), VM(piece_state, BF16),
        VM(piece_state, BF16), VM((2,) + piece_state, BF16),
        VM((2, length, DV), BF16), VM((length, width), F32),
        VM((groups - 1, length, width), BF16), VM((groups - 1, length, width), BF16),
        VM((length, width), BF16),
        dma((6,)), dma((groups,)), dma((groups,)), dma((groups,)), dma((2,)),
        dma((CHUNKS,)), dma((CHUNKS,)), dma((CHUNKS,)), dma((CHUNKS,)),
        dma((CHUNKS,)), dma((CHUNKS,)), dma((pieces,)), dma((pieces,)),
        dma((groups - 1, pieces)), dma((groups - 1, pieces)), dma((pieces,)),
    ]
    return pl.pallas_call(
        functools.partial(kernel, n_seq, n_head),
        out_shape=jax.ShapeDtypeStruct((length, width), BF16),
        in_specs=[pl.BlockSpec(memory_space=pl.ANY)] * 7,
        out_specs=pl.BlockSpec(memory_space=pl.ANY),
        scratch_shapes=scratch,
        compiler_params=pltpu.CompilerParams(
            collective_id=0, has_side_effects=True, vmem_limit_bytes=56 * 2**20
        ),
        name="gated_layer",
    )(queries, key_vectors, values, log_gate, out_gate, norm_gain.reshape(1, DV), out_weight)


def solution(mesh):
    in_specs = (
        P("seq", "head"),
        P("seq", "head"),
        P("seq", "head"),
        P("seq", "head"),
        P("seq", "head"),
        P("head"),
        P("head", None),
    )
    out_specs = P("seq", "head")
    body = functools.partial(shards, mesh.shape["seq"], mesh.shape["head"])
    return jax.shard_map(body, mesh=mesh, in_specs=in_specs, out_specs=out_specs, check_vma=False)
```

time: 147 us -> 38.3 us (0.26)
  the two profiles are of different devices: /device:TPU:26 before, /device:TPU:25 now
where the time goes in v1:
time: 38.3 us; the launch traced here: 38.1 us
  Pallas kernels  36.2 us (95%)
  local copies, waits for them, and re-layouts  1.87 us (5%)
    pallas_call x1, Pallas kernels, shards(): pl.pallas_call(functools.partial(kernel, n_seq, n_head), out_shape=jax.Sh...  36.2 us
    unnamed x1, local copies, waits for them, and re-layouts  1.87 us

profile of v1, /device:TPU:25, one launch (start us, length us, event | category | flops | bytes accessed | tf_op | source)
XLA Modules:
  0.0 38.1 jit_solution(2815566077551949054)
XLA Ops:
  0.0 36.2 %gated_layer.1 = bf16[512,512]{1,0:T(8,128)(2,1)} custom-call(bf16[512,256]{1,0:T(8,128)(2,1)} %q_hbm.1, bf16[512,256]{1,0:T(8,128)(2,1)} %k_hbm.1, bf16[512,512]{1,0:T(8,128)(2,1)} %v_hbm.1, bf16[512,256]{1,0:T(8,128)(2,1)} %g_hbm.1, bf16[512,512]{1,0:T(8,128)(2,1)} %o_hbm.1, f32[1,512]{1,0:T(1,128)} %bitcast.1, bf16[512,2048]{1,0:T(8,128)(2,1)} %w_hbm.1), custom_call_target="tpu_custom_call" | custom-call | tf_op jit(solution)/shard_map/gated_layer/pallas_call | solution.py:293
  36.2 1.9 %copy.9 = bf16[512,512]{1,0:T(8,128)(2,1)} copy(bf16[512,512]{1,0:T(8,128)(2,1)} %gated_layer.1) | data formatting | bytes 1048576

commit v2 on v1

--- a/solution.py
+++ b/solution.py
@@ -10,8 +10,8 @@
 DK = 256
 DV = 512
 SPAN = 64
-CHUNKS = 4
-TOKENS = 128
+CHUNKS = 8
+TOKENS = 64
 F32 = jnp.float32
 BF16 = jnp.bfloat16
 MESH = pl.DeviceIdType.MESH
@@ -24,13 +24,13 @@
 def kernel(
     n_seq, n_head,
     q_hbm, k_hbm, v_hbm, g_hbm, o_hbm, gain_hbm, w_hbm,
-    out_hbm,
+    out,
     q, k, v, g, o, gain, w,
     run, ends, kd, qg, att, act, state,
     log_out, log_in, half_out, half_in, own_half, chain_out, chain_in, pass_out, carry,
-    gated, mine, y_out, y_in, out,
+    gated, mine, y_out, y_in,
     load_sem, w_sem, w_send, w_recv, log_sem, half_send, half_recv,
-    chain_send, chain_recv, pass_send, pass_recv, g_send, g_recv, y_send, y_recv, out_sem,
+    chain_send, chain_recv, pass_send, pass_recv, g_send, g_recv, y_send, y_recv,
 ):
     length = q.shape[0]
     blocks = length // SPAN
@@ -49,6 +49,8 @@
     across = {"seq": seq + 1 - 2 * x, "head": head}
     onward = {"seq": lax.rem(seq + 2, n_seq), "head": head}
     back = {"seq": lax.rem(seq + n_seq - 2, n_seq), "head": head}
+    leads = z < last
+    follows = z > 0
     partner = {"seq": seq, "head": head + 1 - 2 * core}
     peers = [
         {"seq": seq, "head": lax.rem(head + 2 * step, n_head)} for step in range(1, groups)
@@ -72,9 +74,15 @@
         for j in range(groups)
     ]
     barrier = pltpu.get_barrier_semaphore()
-    friends = [across, onward, back, partner] + peers
-    for friend in friends:
+
+    def greet(friend):
         pl.semaphore_signal(barrier, inc=1, device_id=friend, device_id_type=MESH)
+
+    for friend in [across, partner] + peers:
+        greet(friend)
+    pl.when(leads)(lambda: greet(onward))
+    pl.when(follows)(lambda: greet(back))
+    met = 2 + len(peers) + leads.astype(jnp.int32) + follows.astype(jnp.int32)
 
     def remote(src, dst, send, recv, device):
         return pltpu.make_async_remote_copy(
@@ -108,7 +116,7 @@
         kd[part, :] = (k[part, :].astype(F32) * jnp.exp((endings[b] - run[b]) + tail)).astype(BF16)
         tail = tail + endings[b]
 
-    pl.semaphore_wait(barrier, len(friends))
+    pl.semaphore_wait(barrier, met)
     log_copy = remote(log_out, log_in, log_sem.at[0], log_sem.at[1], across)
     log_copy.start()
     loads[2].wait()
@@ -164,7 +172,8 @@
         act[part, :] = of / (1.0 + jnp.exp(-of)) * gain[...]
         return 0
 
-    lax.fori_loop(0, blocks, local, 0)
+    early = jnp.where(leads, blocks // 2, blocks)
+    lax.fori_loop(0, early, local, 0)
 
     log_copy.wait()
     mine_log = log_out[0:1, :]
@@ -185,7 +194,7 @@
         s0 = jnp.where(first, own, other)
         s1 = jnp.where(first, other, own)
 
-        @pl.when(z > 0)
+        @pl.when(follows)
         def _():
             chain.wait_recv()
 
@@ -193,7 +202,7 @@
         between = decay0 * entering + s0
         chain_out[i] = (decay1 * between + s1).astype(BF16)
 
-        @pl.when(z < last)
+        @pl.when(leads)
         def _():
             chain.start()
 
@@ -204,6 +213,7 @@
         )
         passing.start()
         pass_copies.append(passing)
+    lax.fori_loop(early, blocks, local, 0)
     for passing in pass_copies:
         passing.wait_recv()
     carried = carry[...].reshape(DV, DK)
@@ -240,7 +250,6 @@
     for i in range(pieces):
         part = slice(i * TOKENS, (i + 1) * TOKENS)
         mine[part, :] = dot(gated[0, part, :], w[0, 0]) + dot(gated[1, part, :], w[1, 0])
-    stores = []
     for i in range(pieces):
         part = slice(i * TOKENS, (i + 1) * TOKENS)
         total_out = mine[part, :]
@@ -248,19 +257,13 @@
             y_copies[i * (groups - 1) + j - 1].wait_recv()
             total_out = total_out + y_in[j - 1, part, :].astype(F32)
         out[part, :] = total_out.astype(BF16)
-        store = pltpu.make_async_copy(out.at[part, :], out_hbm.at[part, :], out_sem.at[i])
-        store.start()
-        stores.append(store)
     for copy in half_copies + pass_copies + w_copies + g_copies + y_copies:
         copy.wait_send()
 
-    @pl.when(z < last)
+    @pl.when(leads)
     def _():
         for chain in chain_copies:
             chain.wait_send()
-
-    for store in stores:
-        store.wait()
 
 
 def shards(n_seq, n_head, queries, key_vectors, values, log_gate, out_gate, norm_gain, out_weight):
@@ -284,17 +287,16 @@
         VM(piece_state, BF16), VM((2,) + piece_state, BF16),
         VM((2, length, DV), BF16), VM((length, width), F32),
         VM((groups - 1, length, width), BF16), VM((groups - 1, length, width), BF16),
-        VM((length, width), BF16),
         dma((6,)), dma((groups,)), dma((groups,)), dma((groups,)), dma((2,)),
         dma((CHUNKS,)), dma((CHUNKS,)), dma((CHUNKS,)), dma((CHUNKS,)),
         dma((CHUNKS,)), dma((CHUNKS,)), dma((pieces,)), dma((pieces,)),
-        dma((groups - 1, pieces)), dma((groups - 1, pieces)), dma((pieces,)),
+        dma((groups - 1, pieces)), dma((groups - 1, pieces)),
     ]
     return pl.pallas_call(
         functools.partial(kernel, n_seq, n_head),
-        out_shape=jax.ShapeDtypeStruct((length, width), BF16),
+        out_shape=pltpu.VMEM((length, width), BF16),
         in_specs=[pl.BlockSpec(memory_space=pl.ANY)] * 7,
-        out_specs=pl.BlockSpec(memory_space=pl.ANY),
+        out_specs=pl.BlockSpec(memory_space=pltpu.VMEM),
         scratch_shapes=scratch,
         compiler_params=pltpu.CompilerParams(
             collective_id=0, has_side_effects=True, vmem_limit_bytes=56 * 2**20

time: 38.3 us -> 33.5 us (0.87)
  the two profiles are of different devices: /device:TPU:25 before, /device:TPU:26 now
where the time goes in v2:
time: 33.5 us; the launch traced here: 33.4 us
  Pallas kernels  32.6 us (97%)
  local copies, waits for them, and re-layouts  0.8 us (2%)
    pallas_call x1, Pallas kernels, shards(): pl.pallas_call(functools.partial(kernel, n_seq, n_head), out_shape=pltpu....  32.6 us
    unnamed x1, local copies, waits for them, and re-layouts  0.8 us

profile of v2, /device:TPU:26, one launch (start us, length us, event | category | flops | bytes accessed | tf_op | source)
XLA Modules:
  0.0 33.4 jit_solution(13318264942429273446)
XLA Ops:
  0.0 32.6 %gated_layer.1 = bf16[512,512]{1,0:T(8,128)(2,1)S(1)} custom-call(bf16[512,256]{1,0:T(8,128)(2,1)} %q_hbm.1, bf16[512,256]{1,0:T(8,128)(2,1)} %k_hbm.1, bf16[512,512]{1,0:T(8,128)(2,1)} %v_hbm.1, bf16[512,256]{1,0:T(8,128)(2,1)} %g_hbm.1, bf16[512,512]{1,0:T(8,128)(2,1)} %o_hbm.1, f32[1,512]{1,0:T(1,128)} %bitcast.1, bf16[512,2048]{1,0:T(8,128)(2,1)} %w_hbm.1), custom_call_target="tpu_custom_call" | custom-call | tf_op jit(solution)/shard_map/gated_layer/pallas_call | solution.py:295
  32.6 0.8 %copy.9 = bf16[512,512]{1,0:T(8,128)(2,1)} copy(bf16[512,512]{1,0:T(8,128)(2,1)S(1)} %gated_layer.1) | data formatting | bytes 1048576

commit v3 on v2

--- a/solution.py
+++ b/solution.py
@@ -12,6 +12,8 @@
 SPAN = 64
 CHUNKS = 8
 TOKENS = 64
+DETOUR = 1
+HOLD = 6
 F32 = jnp.float32
 BF16 = jnp.bfloat16
 MESH = pl.DeviceIdType.MESH
@@ -28,16 +30,17 @@
     q, k, v, g, o, gain, w,
     run, ends, kd, qg, att, act, state,
     log_out, log_in, half_out, half_in, own_half, chain_out, chain_in, pass_out, carry,
-    gated, mine, y_out, y_in,
+    gated, mine, y_out, y_in, decay, near, far,
     load_sem, w_sem, w_send, w_recv, log_sem, half_send, half_recv,
     chain_send, chain_recv, pass_send, pass_recv, g_send, g_recv, y_send, y_recv,
+    near_send, near_recv, far_send, far_recv, home_send, home_recv,
 ):
     length = q.shape[0]
     blocks = length // SPAN
     pieces = length // TOKENS
     groups = n_head // 2
     width = w_hbm.shape[1] // n_head
-    half = DV // 2
+    half = DK // 2
     rows = half // CHUNKS
     seq = lax.axis_index("seq")
     head = lax.axis_index("head")
@@ -123,7 +126,7 @@
 
     def half_state(which):
         cols = pl.ds(pl.multiple_of(which * half, 128), half)
-        return dot(v[:, cols], kd[...], ((0,), (0,)))
+        return dot(kd[:, cols], v[...], ((0,), (0,)))
 
     theirs = half_state(1 - x).astype(BF16)
     half_copies = []
@@ -132,7 +135,7 @@
         copy = remote(half_out.at[i], half_in.at[i], half_send.at[i], half_recv.at[i], across)
         copy.start()
         half_copies.append(copy)
-    own_half[...] = half_state(x).reshape(CHUNKS, rows, DK)
+    own_half[...] = half_state(x).reshape(CHUNKS, rows, DV)
     for load in w_loads:
         load.start()
     w_copies = [
@@ -148,6 +151,10 @@
     for load in loads[3:]:
         load.wait()
     state[...] = jnp.zeros_like(state)
+
+    def column(row):
+        lanes = jnp.broadcast_to(row, (128, DK)).T
+        return jnp.concatenate([lanes] * (DV // 128), axis=1)
 
     def local(b, _):
         part = pl.ds(pl.multiple_of(b * SPAN, SPAN), SPAN)
@@ -166,8 +173,8 @@
         scores = dot(q_intra, k_intra, ((1,), (1,)))
         weights = jnp.where(tri, scores, 0.0).astype(BF16)
         held = state[...]
-        att[part, :] = dot(weights, vb) + dot(qi.astype(BF16), held.astype(BF16), ((1,), (1,)))
-        state[...] = held * jnp.exp(ending) + dot(vb, k_state, ((0,), (0,)))
+        att[part, :] = dot(weights, vb) + dot(qi.astype(BF16), held.astype(BF16))
+        state[...] = held * column(jnp.exp(ending)) + dot(k_state, vb, ((0,), (0,)))
         of = o[part, :].astype(F32)
         act[part, :] = of / (1.0 + jnp.exp(-of)) * gain[...]
         return 0
@@ -179,8 +186,15 @@
     mine_log = log_out[0:1, :]
     their_log = log_in[0:1, :]
     first = x == 0
-    decay0 = jnp.exp(jnp.where(first, mine_log, their_log))
-    decay1 = jnp.exp(jnp.where(first, their_log, mine_log))
+    for i, logs in enumerate(
+        (jnp.where(first, mine_log, their_log), jnp.where(first, their_log, mine_log))
+    ):
+        decay[i] = jnp.broadcast_to(jnp.exp(logs), (128, DK)).T
+
+    def decays(i, at):
+        lanes = decay[i, pl.ds(pl.multiple_of(x * half + at * rows, rows), rows), :]
+        return jnp.concatenate([lanes] * (DV // 128), axis=1)
+
     chain_copies = []
     pass_copies = []
     for i in range(CHUNKS):
@@ -199,8 +213,8 @@
             chain.wait_recv()
 
         entering = chain_in[i].astype(F32)
-        between = decay0 * entering + s0
-        chain_out[i] = (decay1 * between + s1).astype(BF16)
+        between = decays(0, i) * entering + s0
+        chain_out[i] = (decays(1, i) * between + s1).astype(BF16)
 
         @pl.when(leads)
         def _():
@@ -216,12 +230,12 @@
     lax.fori_loop(early, blocks, local, 0)
     for passing in pass_copies:
         passing.wait_recv()
-    carried = carry[...].reshape(DV, DK)
+    carried = carry[...].reshape(DK, DV)
 
     g_copies = []
     for i in range(pieces):
         part = slice(i * TOKENS, (i + 1) * TOKENS)
-        a = att[part, :] + dot(qg[part, :], carried, ((1,), (1,)))
+        a = att[part, :] + dot(qg[part, :], carried)
         spread = jnp.mean(a * a, axis=-1, keepdims=True)
         gated[0, part, :] = (a * lax.rsqrt(spread + 1e-05) * act[part, :]).astype(BF16)
         copy = remote(
@@ -233,30 +247,87 @@
         copy.wait()
     for copy in w_copies:
         copy.wait_recv()
-    y_copies = []
+    first_pair = z == 0
+    direct, nears, fars, homes = {}, {}, {}, {}
+    for j in range(groups - 1):
+        for i in range(pieces):
+            part = slice(i * TOKENS, (i + 1) * TOKENS)
+            direct[i, j] = remote(
+                y_out.at[j, part, :], y_in.at[j, part, :],
+                y_send.at[j, i], y_recv.at[j, i], peers[j],
+            )
+            if i < DETOUR:
+                nears[i, j] = remote(
+                    y_out.at[j, part, :], near.at[j, i],
+                    near_send.at[j, i], near_recv.at[j, i], back,
+                )
+                fars[i, j] = remote(
+                    near.at[j, i], far.at[j, i], far_send.at[j, i], far_recv.at[j, i], peers[j]
+                )
+                homes[i, j] = remote(
+                    far.at[j, i], y_in.at[j, part, :],
+                    home_send.at[j, i], home_recv.at[j, i], onward,
+                )
+    detours = sorted(nears)
     for i in range(pieces):
         part = slice(i * TOKENS, (i + 1) * TOKENS)
         g_copies[i].wait_recv()
-        for j in range(1, groups):
-            y_out[j - 1, part, :] = (
-                dot(gated[0, part, :], w[0, j]) + dot(gated[1, part, :], w[1, j])
+        if i == HOLD:
+
+            @pl.when(leads)
+            def _():
+                for at in detours:
+                    nears[at].wait_recv()
+                    fars[at].start()
+
+        for j in range(groups - 1):
+            y_out[j, part, :] = (
+                dot(gated[0, part, :], w[0, j + 1]) + dot(gated[1, part, :], w[1, j + 1])
             ).astype(BF16)
-            copy = remote(
-                y_out.at[j - 1, part, :], y_in.at[j - 1, part, :],
-                y_send.at[j - 1, i], y_recv.at[j - 1, i], peers[j - 1],
-            )
-            copy.start()
-            y_copies.append(copy)
+            if i < DETOUR:
+                pl.when(follows)(nears[i, j].start)
+                pl.when(first_pair)(direct[i, j].start)
+            else:
+                direct[i, j].start()
     for i in range(pieces):
         part = slice(i * TOKENS, (i + 1) * TOKENS)
         mine[part, :] = dot(gated[0, part, :], w[0, 0]) + dot(gated[1, part, :], w[1, 0])
-    for i in range(pieces):
+
+    @pl.when(leads)
+    def _():
+        for at in detours:
+            fars[at].wait_recv()
+            homes[at].start()
+
+    for i in list(range(DETOUR, pieces)) + list(range(DETOUR)):
         part = slice(i * TOKENS, (i + 1) * TOKENS)
         total_out = mine[part, :]
-        for j in range(1, groups):
-            y_copies[i * (groups - 1) + j - 1].wait_recv()
-            total_out = total_out + y_in[j - 1, part, :].astype(F32)
+        for j in range(groups - 1):
+            if i < DETOUR:
+                pl.when(follows)(homes[i, j].wait_recv)
+                pl.when(first_pair)(direct[i, j].wait_recv)
+            else:
+                direct[i, j].wait_recv()
+            total_out = total_out + y_in[j, part, :].astype(F32)
         out[part, :] = total_out.astype(BF16)
+
+    @pl.when(follows)
+    def _():
+        for at in detours:
+            nears[at].wait_send()
+
+    @pl.when(first_pair)
+    def _():
+        for at in detours:
+            direct[at].wait_send()
+
+    @pl.when(leads)
+    def _():
+        for at in detours:
+            fars[at].wait_send()
+            homes[at].wait_send()
+
+    y_copies = [direct[at] for at in direct if at not in nears]
     for copy in half_copies + pass_copies + w_copies + g_copies + y_copies:
         copy.wait_send()
 
@@ -272,25 +343,28 @@
     groups = n_head // 2
     blocks = length // SPAN
     pieces = length // TOKENS
-    half_rows = DV // 2 // CHUNKS
+    half_rows = DK // 2 // CHUNKS
     VM = pltpu.VMEM
     dma = pltpu.SemaphoreType.DMA
-    piece_state = (CHUNKS, half_rows, DK)
+    piece_state = (CHUNKS, half_rows, DV)
     scratch = [
         VM((length, DK), BF16), VM((length, DK), BF16), VM((length, DV), BF16),
         VM((length, DK), BF16), VM((length, DV), BF16), VM((1, DV), F32),
         VM((2, groups, DV, width), BF16),
         VM((blocks, SPAN, DK), F32), VM((blocks, DK), F32), VM((length, DK), BF16),
-        VM((length, DK), BF16), VM((length, DV), F32), VM((length, DV), F32), VM((DV, DK), F32),
+        VM((length, DK), BF16), VM((length, DV), F32), VM((length, DV), F32), VM((DK, DV), F32),
         VM((8, DK), F32), VM((8, DK), F32), VM(piece_state, BF16), VM(piece_state, BF16),
         VM(piece_state, F32), VM(piece_state, BF16), VM(piece_state, BF16),
         VM(piece_state, BF16), VM((2,) + piece_state, BF16),
         VM((2, length, DV), BF16), VM((length, width), F32),
         VM((groups - 1, length, width), BF16), VM((groups - 1, length, width), BF16),
+        VM((2, DK, 128), F32),
+        VM((groups - 1, DETOUR, TOKENS, width), BF16), VM((groups - 1, DETOUR, TOKENS, width), BF16),
         dma((6,)), dma((groups,)), dma((groups,)), dma((groups,)), dma((2,)),
         dma((CHUNKS,)), dma((CHUNKS,)), dma((CHUNKS,)), dma((CHUNKS,)),
         dma((CHUNKS,)), dma((CHUNKS,)), dma((pieces,)), dma((pieces,)),
         dma((groups - 1, pieces)), dma((groups - 1, pieces)),
+    ] + [dma((groups - 1, DETOUR))] * 6 + [
     ]
     return pl.pallas_call(
         functools.partial(kernel, n_seq, n_head),

time: 33.5 us -> 32.5 us (0.970)
  Pallas kernels: 32.6 us -> 31.6 us
    pallas_call x1, Pallas kernels: 32.6 us -> 31.6 us  [shards(): pl.pallas_call(functools.partial(kernel, n_seq, n_head), out_shape=pltpu....]
where the time goes in v3:
time: 32.5 us; the launch traced here: 32.4 us
  Pallas kernels  31.6 us (97%)
  local copies, waits for them, and re-layouts  0.8 us (2%)
    pallas_call x1, Pallas kernels, shards(): pl.pallas_call(functools.partial(kernel, n_seq, n_head), out_shape=pltpu....  31.6 us
    unnamed x1, local copies, waits for them, and re-layouts  0.8 us

profile of v3, /device:TPU:26, one launch (start us, length us, event | category | flops | bytes accessed | tf_op | source)
XLA Modules:
  0.0 32.4 jit_solution(13181250913660105852)
XLA Ops:
  0.0 31.6 %gated_layer.1 = bf16[512,512]{1,0:T(8,128)(2,1)S(1)} custom-call(bf16[512,256]{1,0:T(8,128)(2,1)} %q_hbm.1, bf16[512,256]{1,0:T(8,128)(2,1)} %k_hbm.1, bf16[512,512]{1,0:T(8,128)(2,1)} %v_hbm.1, bf16[512,256]{1,0:T(8,128)(2,1)} %g_hbm.1, bf16[512,512]{1,0:T(8,128)(2,1)} %o_hbm.1, f32[1,512]{1,0:T(1,128)} %bitcast.1, bf16[512,2048]{1,0:T(8,128)(2,1)} %w_hbm.1), custom_call_target="tpu_custom_call" | custom-call | tf_op jit(solution)/shard_map/gated_layer/pallas_call | solution.py:369
  31.6 0.8 %copy.9 = bf16[512,512]{1,0:T(8,128)(2,1)} copy(bf16[512,512]{1,0:T(8,128)(2,1)S(1)} %gated_layer.1) | data formatting | bytes 1048576
